TPU v7x, 32 devices: a whole 2x2x4 slice. The times are simulated.
32 devices in a mesh: grp: 2 (over x), pool: 16 (over z, y, core).
Axes of the slice: x: 2, y: 2, z: 4, core: 2. Of those that a mesh axis runs over, the one named last changes fastest.
Arguments:
- query: bfloat16 [32, 4096], P(('grp', 'pool')), parts along dimension 0, may hold values from -6 to 6
- kv_pool: bfloat16 [2048, 2, 16, 512], P(('grp', 'pool')), parts along dimension 0, may hold values from -6 to 6
- holder_table: int32 [32, 128], P(('grp', 'pool')), parts along dimension 0, may hold values from 0 to 15, as said below
- slot_table: int32 [32, 128], P(('grp', 'pool')), parts along dimension 0, may hold values from 0 to 63
- lengths: int32 [32], P(('grp', 'pool')), parts along dimension 0, may hold values from 96 to 128, as said below
- out_weight: bfloat16 [4096, 8192], P('pool'), may hold values from -1.1953125 to 1.1953125
Outputs:
- mixed: bfloat16 [32, 8192], P(('grp', 'pool')), parts along dimension 0
There are 2 independent parts, one for each index of `grp`. A program takes and returns all parts, laid end to end along the dimension named above; an argument that names none is the same for every part. Nothing has to cross between parts.
Inputs may be any that keep to these rules, and one draw needn't show every extreme that they name: `holder_table`: entry [r, j] is the index along pool of the device holding block j of request r. Of one request's 128 blocks at most 16 have the same holder, and some holder has exactly 16 of the request's first 96 blocks. Request r's live blocks are 0 to lengths[r] - 1; some request has 128.
All inputs are finite; a program needn't handle non-finite values.
Results may differ from a plain program's by a relative error of at most 0.0053.
Values may be sent and summed in bfloat16 or wider, within the bound.
A program may use at most 64 MiB of HBM per device.

v0:
```python
import math
import jax
import jax.numpy as jnp
from jax import lax
from jax.sharding import PartitionSpec as P

H = 32
KVH = 4
HD = 128
lowest = -1e30


def block_partials(query_heads, kv_blocks):
    head_dim = query_heads.shape[-1]
    kv_heads = query_heads.shape[1]
    block_len = kv_blocks.shape[3]
    block_shape = kv_blocks.shape[:2] + (block_len, kv_heads, head_dim)
    key_part = kv_blocks[:, :, 0].reshape(block_shape)
    value_part = kv_blocks[:, :, 1].reshape(block_shape)
    scores = jnp.einsum(
        "agqd,acbgd->acgqb", query_heads, key_part, preferred_element_type=jnp.float32
    )
    scores = scores * (1.0 / math.sqrt(head_dim))
    maxima = jnp.max(scores, axis=-1)
    shifted = jnp.exp(scores - maxima[..., None])
    totals = jnp.sum(shifted, axis=-1)
    outputs = jnp.einsum(
        "acgqb,acbgd->acgqd",
        shifted.astype(jnp.bfloat16),
        value_part,
        preferred_element_type=jnp.float32,
    )
    return (maxima, outputs, totals)


def merge_blocks(maxima, outputs, totals, live_mask, axis_pos):
    peak_score = jnp.max(jnp.where(live_mask, maxima, lowest), axis=axis_pos, keepdims=True)
    factor = jnp.exp(jnp.where(live_mask, maxima - peak_score, lowest))
    numerator = jnp.sum(factor[..., None] * outputs, axis=axis_pos)
    denominator = jnp.sum(factor * totals, axis=axis_pos)
    return (jnp.squeeze(peak_score, axis_pos), numerator, denominator)


def per_device(query, kv_pool, holder_table, slot_table, lengths, out_weight):
    pool_size = lax.axis_size("pool")
    my_index = lax.axis_index("pool")
    max_blocks = holder_table.shape[1]
    capacity = 2 * max_blocks // pool_size
    groups = H // KVH
    all_holders, all_slots, all_lengths = (
        lax.all_gather(holder_table, "pool", axis=0, tiled=True),
        lax.all_gather(slot_table, "pool", axis=0, tiled=True),
        lax.all_gather(lengths, "pool", axis=0, tiled=True),
    )
    cap_iota = jnp.arange(capacity, dtype=jnp.int32)
    block_iota = jnp.arange(max_blocks, dtype=jnp.int32)
    held_here = all_holders == my_index
    rank_here = jnp.cumsum(held_here.astype(jnp.int32), axis=1) - 1
    pick_hot = held_here[:, None, :] & (rank_here[:, None, :] == cap_iota[None, :, None])
    pick_slot = jnp.sum(jnp.where(pick_hot, all_slots[:, None, :], 0), axis=-1)
    pick_block = jnp.sum(jnp.where(pick_hot, block_iota[None, None, :], 0), axis=-1)
    send_live = jnp.any(pick_hot, axis=-1) & (pick_block < all_lengths[:, None])
    send_blocks = kv_pool[pick_slot]
    all_queries = lax.all_gather(query, "pool", axis=0, tiled=True)
    maxima, outputs, totals = block_partials(
        all_queries.reshape(pool_size, KVH, groups, HD), send_blocks
    )
    part_peak, part_numer, part_denom = merge_blocks(
        maxima, outputs, totals, send_live[:, :, None, None], 1
    )
    got_peak, got_numer, got_denom = (
        lax.all_to_all(
            part_peak.reshape(pool_size, H), "pool", split_axis=0, concat_axis=0, tiled=True
        ),
        lax.all_to_all(
            part_numer.reshape(pool_size, H * HD), "pool", split_axis=0, concat_axis=0, tiled=True
        ),
        lax.all_to_all(
            part_denom.reshape(pool_size, H), "pool", split_axis=0, concat_axis=0, tiled=True
        ),
    )
    peak_score, numerator, denominator = merge_blocks(
        got_peak.reshape(pool_size, KVH, groups),
        got_numer.reshape(pool_size, KVH, groups, HD),
        got_denom.reshape(pool_size, KVH, groups),
        True,
        0,
    )
    attention = (numerator / denominator[..., None]).reshape(1, H * HD).astype(jnp.bfloat16)
    features = lax.all_to_all(attention, "pool", split_axis=1, concat_axis=0, tiled=True)
    return lax.psum_scatter(
        jnp.dot(features, out_weight, preferred_element_type=jnp.float32),
        "pool",
        scatter_dimension=0,
        tiled=True,
    ).astype(jnp.bfloat16)


def solution(mesh):
    placed = (
        P(("grp", "pool"), None),
        P(("grp", "pool"), None, None, None),
        P(("grp", "pool"), None),
        P(("grp", "pool"), None),
        P(("grp", "pool")),
        P("pool", None),
    )
    return jax.shard_map(
        per_device, mesh=mesh, in_specs=placed, out_specs=P(("grp", "pool"), None), check_vma=False
    )
```

profile of v0, /device:TPU:0, one launch (start us, length us, event | category | flops | bytes accessed | tf_op | source)
XLA Modules:
  0.0 231.0 jit_solution(6533422985778512869)
XLA Ops:
  0.0 0.0 copy-start
  0.0 23.4 %all-gather = s32[16,1,128]{2,1,0:T(1,128)S(1)} all-gather(s32[1,1,128]{2,1,0:T(1,128)} %bitcast.78), channel_id=1, replica_groups=mesh['grp'=2,'pool'=16] {'pool'}, dimensions={0}, use_global_device_ids=true | all-gather | bytes 8704 | tf_op jit(solution)/shard_map/all_gather | solution.py:51
  23.4 0.3 reduce_window_sum.11
  23.7 17.6 %all-gather.1 = s32[16,1,128]{2,1,0:T(1,128)S(1)} all-gather(s32[1,1,128]{2,1,0:T(1,128)} %bitcast.79), channel_id=1, replica_groups=mesh['grp'=2,'pool'=16] {'pool'}, dimensions={0}, use_global_device_ids=true | all-gather | bytes 8704 | tf_op jit(solution)/shard_map/all_gather | solution.py:52
  42.0 0.6 select_reduce_fusion.2
  42.6 1.3 fusion.18
  43.9 0.8 dynamic-update-slice
  44.7 0.4 fusion.12
  45.0 9.4 %all-reduce = s32[16]{0:T(128)S(1)} all-reduce(s32[16]{0:T(128)S(1)} %dynamic-update-slice), channel_id=1, replica_groups=mesh['grp'=2,'pool'=16] {'pool'}, use_global_device_ids=true, to_apply=%add | all-reduce | flops 16 | bytes 128
  54.4 0.1 reshape.132
  54.5 0.0 copy-done
  54.5 8.5 %gather_fusion = bf16[256,2,16,512]{3,2,1,0:T(8,128)(2,1)} fusion(bf16[64,2,16,512]{3,2,1,0:T(8,128)(2,1)S(1)} %copy-done, s32[1024]{0:T(1024)S(1)} %pad_clamp_fusion), kind=kCustom, calls=%fused_computation | custom fusion | bytes 16778240 | tf_op jit(solution)/shard_map/gather | solution.py:63
  63.0 6.1 %slice_bitcast_fusion = (bf16[16,16,1,16,512]{4,3,1,0,2:T(8,128)(2,1)}, bf16[16,16,1,16,512]{4,3,1,0,2:T(8,128)(2,1)}) fusion(bf16[16,16,2,16,512]{4,3,2,1,0:T(8,128)(2,1)} %bitcast.64), kind=kLoop, calls=%fused_computation.1 | loop fusion | bytes 16777216
  69.1 6.9 %reshape_squeeze.6 = bf16[16,16,16,4,128]{4,3,2,1,0:T(4,128)(2,1)} reshape(bf16[16,16,1,16,512]{4,3,1,0,2:T(8,128)(2,1)} %get-tuple-element.12) | data formatting | bytes 8388608 | tf_op jit(solution)/shard_map/reshape;squeeze | solution.py:18
  76.0 21.5 %all-gather.2 = bf16[16,1,4096]{2,1,0:T(2,128)(2,1)S(1)} all-gather(bf16[1,1,4096]{2,1,0:T(2,128)(2,1)S(1)} %bitcast.77), channel_id=1, replica_groups=mesh['grp'=2,'pool'=16] {'pool'}, dimensions={0}, use_global_device_ids=true | all-gather | bytes 139264 | tf_op jit(solution)/shard_map/all_gather | solution.py:64
  97.5 0.7 reduce.6
  98.3 12.2 %bitcast_reduce_fusion = (f32[16,16,4,8]{3,1,2,0:T(8,128)S(1)}, f32[16,4,16,16,8]{3,4,2,1,0:T(8,128)S(1)}) fusion(bf16[16,4,8,128,1]{3,2,1,0,4:T(8,128)(2,1)S(1)} %bitcast.66, bf16[16,16,16,4,128]{4,3,2,1,0:T(4,128)(2,1)} %reshape_squeeze.6), kind=kOutput, calls=%fused_computation.4 | convolution fusion | flops 33808384 | bytes 4882432 | tf_op jit(solution)/shard_map/agqd,acbgd->acgqb/dot_general | solution.py:20
  110.4 0.1 compare_and_fusion
  110.5 0.2 select_reduce_fusion
  110.7 2.9 %fusion.5 = (f32[16,16,4,8]{3,1,2,0:T(8,128)S(1)}, bf16[16,16,4,8,16]{4,3,1,2,0:T(8,128)(2,1)}) fusion(f32[16,4,16,16,8]{3,4,2,1,0:T(8,128)S(1)} %get-tuple-element.18, f32[16,16,4,8]{3,1,2,0:T(8,128)S(1)} %get-tuple-element.17), kind=kLoop, calls=%fused_computation.11 | loop fusion | flops 516096 | bytes 851968 | tf_op jit(solution)/shard_map/reduce_sum | solution.py:26
  113.6 0.3 multiply_reduce_fusion.1
  113.9 0.1 copy.54
  114.0 0.7 copy.55
  114.7 3.4 %all-to-all-start.2 = ((f32[16,1,32]{2,1,0:T(1,128)}), f32[16,1,32]{2,1,0:T(1,128)S(1)}, u32[]{:S(2)}, u32[]{:S(2)}) async-start(f32[16,1,32]{2,1,0:T(1,128)} %copy.55), calls=%async_computation.2 | async-start | bytes 16384 | tf_op jit(solution)/shard_map/all_to_all | solution.py:78
  118.1 0.1 copy.46
  118.2 0.7 copy.47
  118.9 0.2 copy.50
  119.1 6.9 %reshape_squeeze.7 = bf16[16,16,16,4,128]{4,3,2,1,0:T(4,128)(2,1)} reshape(bf16[16,16,1,16,512]{4,3,1,0,2:T(8,128)(2,1)} %get-tuple-element.11) | data formatting | bytes 8388608 | tf_op jit(solution)/shard_map/reshape;squeeze | solution.py:19
  126.0 0.0 all-to-all-done.2
  126.0 6.0 %all-to-all-start = ((f32[16,1,32]{2,1,0:T(1,128)}), f32[16,1,32]{2,1,0:T(1,128)S(1)}, u32[]{:S(2)}, u32[]{:S(2)}) async-start(f32[16,1,32]{2,1,0:T(1,128)} %copy.47), calls=%async_computation | async-start | bytes 16384 | tf_op jit(solution)/shard_map/all_to_all | solution.py:72
  132.0 5.0 %multiply_reduce_fusion = f32[16,4,8,128]{3,2,1,0:T(8,128)} fusion(bf16[16,16,16,4,128]{4,3,2,1,0:T(4,128)(2,1)} %reshape_squeeze.7, bf16[16,16,4,8,16]{4,3,1,2,0:T(8,128)(2,1)} %get-tuple-element.14, f32[16,16,4,8]{3,2,1,0:T(4,128)S(1)} %copy.50), kind=kOutput, calls=%fused_computation.10 | convolution fusion | flops 35586048 | bytes 4751360 | tf_op jit(solution)/shard_map/acgqb,acbgd->acgqd/dot_general | solution.py:27
  137.0 1.3 all-to-all-done
  138.3 4.7 %all-to-all-start.1 = ((f32[16,1,4096]{2,1,0:T(1,128)}), f32[16,1,4096]{2,1,0:T(1,128)S(1)}, u32[]{:S(2)}, u32[]{:S(2)}) async-start(f32[16,1,4096]{2,1,0:T(1,128)} %bitcast.14), calls=%async_computation.1 | async-start | bytes 524288 | tf_op jit(solution)/shard_map/all_to_all | solution.py:75
  143.1 0.1 sub.44
  143.2 0.1 div.21
  143.3 0.1 copy.48
  143.3 0.1 fusion.13
  143.4 0.1 copy.49
  143.5 9.5 %all-to-all-done.1 = f32[16,1,4096]{2,1,0:T(1,128)S(1)} async-done(((f32[16,1,4096]{2,1,0:T(1,128)}), f32[16,1,4096]{2,1,0:T(1,128)S(1)}, u32[]{:S(2)}, u32[]{:S(2)}) %all-to-all-start.1) | async-done | bytes 262176 | tf_op jit(solution)/shard_map/all_to_all | solution.py:75
  153.0 0.1 mul.40
  153.2 0.3 multiply_reduce_fusion.2
  153.5 0.1 div.22
  153.6 0.5 broadcast.73
  154.1 0.7 reduce.7
  154.8 9.1 %all_to_all.46 = bf16[16,2,128]{2,1,0:T(2,128)(2,1)S(1)} all-to-all(bf16[16,2,128]{2,1,0:T(2,128)(2,1)S(1)} %reshape.157), channel_id=1, replica_groups=mesh['grp'=2,'pool'=16] {'pool'}, dimensions={0} | all-to-all | bytes 16384 | tf_op jit(solution)/shard_map/all_to_all | solution.py:90
  163.9 2.8 %fusion.14 = f32[16,8192]{1,0:T(8,128)S(1)} fusion(bf16[256,8192]{1,0:T(8,128)(2,1)} %param.11, bf16[1,16,256]{2,0,1:T(2,128)(2,1)S(1)} %bitcast.73), kind=kOutput, calls=%fused_computation.29 | convolution fusion | flops 67108864 | bytes 4726784 | tf_op jit(solution)/shard_map/dot_general | solution.py:92
  166.8 63.0 %all-reduce.3 = bf16[16,8192]{1,0:T(8,128)(2,1)S(1)} all-reduce(f32[16,8192]{1,0:T(8,128)S(1)} %fusion.14), channel_id=2, replica_groups=mesh['grp'=2,'pool'=16] {'pool'}, use_global_device_ids=true, to_apply=%region_12.13.clone | all-reduce | flops 131072 | bytes 786432
  229.8 1.2 dynamic-slice_convert_fusion
  (13 shorter events, 0.2 us)
Async XLA Ops:
  0.0 54.5 %copy-start = (bf16[64,2,16,512]{3,2,1,0:T(8,128)(2,1)S(1)}, bf16[64,2,16,512]{3,2,1,0:T(8,128)(2,1)}, u32[]{:S(2)}) copy-start(bf16[64,2,16,512]{3,2,1,0:T(8,128)(2,1)} %param.7) | copy-start | bytes 6291460
  69.1 6.9 %copy-start.1 = (bf16[1,4096]{1,0:T(2,128)(2,1)S(1)}, bf16[1,4096]{1,0:T(2,128)(2,1)}, u32[]{:S(2)}) copy-start(bf16[1,4096]{1,0:T(2,128)(2,1)} %param.6) | copy-start | bytes 24580
  114.7 11.3 %all-to-all-start.2 = ((f32[16,1,32]{2,1,0:T(1,128)}), f32[16,1,32]{2,1,0:T(1,128)S(1)}, u32[]{:S(2)}, u32[]{:S(2)}) async-start(f32[16,1,32]{2,1,0:T(1,128)} %copy.55), calls=%async_computation.2 | async-start | bytes 16384 | tf_op jit(solution)/shard_map/all_to_all | solution.py:78
  126.0 12.3 %all-to-all-start = ((f32[16,1,32]{2,1,0:T(1,128)}), f32[16,1,32]{2,1,0:T(1,128)S(1)}, u32[]{:S(2)}, u32[]{:S(2)}) async-start(f32[16,1,32]{2,1,0:T(1,128)} %copy.47), calls=%async_computation | async-start | bytes 16384 | tf_op jit(solution)/shard_map/all_to_all | solution.py:72
  138.3 14.7 %all-to-all-start.1 = ((f32[16,1,4096]{2,1,0:T(1,128)}), f32[16,1,4096]{2,1,0:T(1,128)S(1)}, u32[]{:S(2)}, u32[]{:S(2)}) async-start(f32[16,1,4096]{2,1,0:T(1,128)} %bitcast.14), calls=%async_computation.1 | async-start | bytes 524288 | tf_op jit(solution)/shard_map/all_to_all | solution.py:75
where the time goes:
time: 232 us; the launch traced here: 231 us
  blocking collectives  144 us (62%)
  local copies, waits for them, and re-layouts  34.6 us (15%)
  matrix products  20 us (9%)
  starting transfers between devices  14.1 us (6%)
  waiting for transfers between devices  10.9 us (5%)
  other arithmetic  6.65 us (3%)
    unnamed x2, blocking collectives  72.4 us
    all_gather x1, blocking collectives, per_device(): lax.all_gather(holder_table, 'pool', axis=0, tiled=True)  23.4 us
    all_gather x1, blocking collectives, per_device(): all_queries = lax.all_gather(query, 'pool', axis=0, tiled=True)  21.5 us
    all_gather x1, blocking collectives, per_device(): lax.all_gather(slot_table, 'pool', axis=0, tiled=True)  17.6 us
    dot_general x1, matrix products, block_partials(): jnp.einsum('agqd,acbgd->acgqb', query_heads, key_part, preferred_element_...  12.2 us
    all_to_all x1, waiting for transfers between devices, per_device(): lax.all_to_all(part_numer.reshape(pool_size, H * HD), 'pool', split_axis=...  9.54 us
    all_to_all x1, blocking collectives, per_device(): lax.all_to_all(attention, 'pool', split_axis=1, concat_axis=0, tiled=True)  9.11 us
    unnamed x12, local copies, waits for them, and re-layouts  8.72 us
  transfers between devices with their start and end apart: 3, of which 2 were waited for; matrix products, arithmetic and copies ran while one was open for 6% of the time, Pallas kernels for 0%

commit v1 on v0

--- a/solution.py
+++ b/solution.py
@@ -61,7 +61,12 @@
     pick_block = jnp.sum(jnp.where(pick_hot, block_iota[None, None, :], 0), axis=-1)
     send_live = jnp.any(pick_hot, axis=-1) & (pick_block < all_lengths[:, None])
     send_blocks = kv_pool[pick_slot]
-    all_queries = lax.all_gather(query, "pool", axis=0, tiled=True)
+    ring = [query]
+    for hop in range(15):
+        ring.append(lax.ppermute(ring[-1], "pool", [(dev, (dev + 1) % 16) for dev in range(16)]))
+    all_queries = jnp.roll(
+        jnp.concatenate(ring[::-1], axis=0), (lax.axis_index("pool") + 1) * ring[0].shape[0], axis=0
+    )
     maxima, outputs, totals = block_partials(
         all_queries.reshape(pool_size, KVH, groups, HD), send_blocks
     )

time: 232 us -> 264 us (1.14)
  waiting for transfers between devices: 10.9 us -> 63 us
  blocking collectives: 144 us -> 121 us
  starting transfers between devices: 14.1 us -> 17.4 us
    ppermute x0 -> x15, waiting for transfers between devices: none -> 52.2 us  [per_device(): lax.ppermute(ring[-1], 'pool', [(dev, (dev + 1) % 16) for dev in range(16)])]
    all_gather x1 -> x0, blocking collectives: 21.5 us -> none  [per_device(): all_queries = lax.all_gather(query, 'pool', axis=0, tiled=True)]
    all_gather x1, blocking collectives: 23.4 us -> 18.2 us  [per_device(): lax.all_gather(holder_table, 'pool', axis=0, tiled=True)]
    unnamed x2, blocking collectives: 72.4 us -> 75.5 us
    unnamed x12 -> x15, local copies, waits for them, and re-layouts: 8.72 us -> 8.07 us
  transfers between devices with their start and end apart: 3 -> 18, of which waited for: 2 -> 11; matrix products, arithmetic and copies ran while one was open for 6% -> 14% of each run, Pallas kernels for 0% -> 0%
where the time goes in v1:
time: 264 us; the launch traced here: 263 us
  blocking collectives  121 us (46%)
  waiting for transfers between devices  63 us (24%)
  local copies, waits for them, and re-layouts  34.8 us (13%)
  matrix products  20 us (8%)
  starting transfers between devices  17.4 us (7%)
  other arithmetic  5.91 us (2%)
    unnamed x2, blocking collectives  75.5 us
    ppermute x15, waiting for transfers between devices, per_device(): lax.ppermute(ring[-1], 'pool', [(dev, (dev + 1) % 16) for dev in range(16)])  52.2 us
    all_gather x1, blocking collectives, per_device(): lax.all_gather(holder_table, 'pool', axis=0, tiled=True)  18.2 us
    all_gather x1, blocking collectives, per_device(): lax.all_gather(slot_table, 'pool', axis=0, tiled=True)  18.2 us
    dot_general x1, matrix products, block_partials(): jnp.einsum('agqd,acbgd->acgqb', query_heads, key_part, preferred_element_...  12.2 us
    all_to_all x1, waiting for transfers between devices, per_device(): lax.all_to_all(part_numer.reshape(pool_size, H * HD), 'pool', split_axis=...  9.54 us
    all_to_all x1, blocking collectives, per_device(): lax.all_to_all(attention, 'pool', split_axis=1, concat_axis=0, tiled=True)  9.11 us
    gather x1, local copies, waits for them, and re-layouts, per_device(): send_blocks = kv_pool[pick_slot]  8.47 us
  transfers between devices with their start and end apart: 18, of which 11 were waited for; matrix products, arithmetic and copies ran while one was open for 14% of the time, Pallas kernels for 0%

profile of v1, /device:TPU:0, one launch (start us, length us, event | category | flops | bytes accessed | tf_op | source)
XLA Modules:
  0.0 263.0 jit_solution(13171096648786176837)
XLA Ops:
  0.0 0.5 collective-permute-start
  0.5 6.6 %collective-permute-done = bf16[1,4096]{1,0:T(2,128)(2,1)S(1)} collective-permute-done((bf16[1,4096]{1,0:T(2,128)(2,1)}, bf16[1,4096]{1,0:T(2,128)(2,1)S(1)}, u32[]{:S(2)}, u32[]{:S(2)}) %collective-permute-start) | collective-permute-done | bytes 8224 | tf_op jit(solution)/shard_map/ppermute | solution.py:66
  7.1 5.9 %collective-permute-done.1 = bf16[1,4096]{1,0:T(2,128)(2,1)S(1)} collective-permute-done((bf16[1,4096]{1,0:T(2,128)(2,1)S(1)}, bf16[1,4096]{1,0:T(2,128)(2,1)S(1)}, u32[]{:S(2)}, u32[]{:S(2)}) %collective-permute-start.1) | collective-permute-done | bytes 8224 | tf_op jit(solution)/shard_map/ppermute | solution.py:66
  13.0 5.9 %collective-permute-done.2 = bf16[1,4096]{1,0:T(2,128)(2,1)S(1)} collective-permute-done((bf16[1,4096]{1,0:T(2,128)(2,1)S(1)}, bf16[1,4096]{1,0:T(2,128)(2,1)S(1)}, u32[]{:S(2)}, u32[]{:S(2)}) %collective-permute-start.2) | collective-permute-done | bytes 8224 | tf_op jit(solution)/shard_map/ppermute | solution.py:66
  18.8 5.9 %collective-permute-done.3 = bf16[1,4096]{1,0:T(2,128)(2,1)S(1)} collective-permute-done((bf16[1,4096]{1,0:T(2,128)(2,1)S(1)}, bf16[1,4096]{1,0:T(2,128)(2,1)S(1)}, u32[]{:S(2)}, u32[]{:S(2)}) %collective-permute-start.3) | collective-permute-done | bytes 8224 | tf_op jit(solution)/shard_map/ppermute | solution.py:66
  24.7 5.9 %collective-permute-done.4 = bf16[1,4096]{1,0:T(2,128)(2,1)S(1)} collective-permute-done((bf16[1,4096]{1,0:T(2,128)(2,1)S(1)}, bf16[1,4096]{1,0:T(2,128)(2,1)S(1)}, u32[]{:S(2)}, u32[]{:S(2)}) %collective-permute-start.4) | collective-permute-done | bytes 8224 | tf_op jit(solution)/shard_map/ppermute | solution.py:66
  30.6 5.9 %collective-permute-done.5 = bf16[1,4096]{1,0:T(2,128)(2,1)S(1)} collective-permute-done((bf16[1,4096]{1,0:T(2,128)(2,1)S(1)}, bf16[1,4096]{1,0:T(2,128)(2,1)S(1)}, u32[]{:S(2)}, u32[]{:S(2)}) %collective-permute-start.5) | collective-permute-done | bytes 8224 | tf_op jit(solution)/shard_map/ppermute | solution.py:66
  36.4 18.2 %all-gather = s32[16,1,128]{2,1,0:T(1,128)S(1)} all-gather(s32[1,1,128]{2,1,0:T(1,128)} %bitcast.76), channel_id=1, replica_groups=mesh['grp'=2,'pool'=16] {'pool'}, dimensions={0}, use_global_device_ids=true | all-gather | bytes 8704 | tf_op jit(solution)/shard_map/all_gather | solution.py:51
  54.6 0.2 collective-permute-start.7
  54.8 0.3 reduce_window_sum.11
  55.0 5.4 %collective-permute-done.7 = bf16[1,4096]{1,0:T(2,128)(2,1)S(1)} collective-permute-done((bf16[1,4096]{1,0:T(2,128)(2,1)S(1)}, bf16[1,4096]{1,0:T(2,128)(2,1)S(1)}, u32[]{:S(2)}, u32[]{:S(2)}) %collective-permute-start.7) | collective-permute-done | bytes 8224 | tf_op jit(solution)/shard_map/ppermute | solution.py:66
  60.5 18.2 %all-gather.1 = s32[16,1,128]{2,1,0:T(1,128)S(1)} all-gather(s32[1,1,128]{2,1,0:T(1,128)} %bitcast.77), channel_id=1, replica_groups=mesh['grp'=2,'pool'=16] {'pool'}, dimensions={0}, use_global_device_ids=true | all-gather | bytes 8704 | tf_op jit(solution)/shard_map/all_gather | solution.py:52
  78.6 0.2 collective-permute-start.9
  78.8 0.6 select_reduce_fusion.2
  79.4 5.1 %collective-permute-done.9 = bf16[1,4096]{1,0:T(2,128)(2,1)S(1)} collective-permute-done((bf16[1,4096]{1,0:T(2,128)(2,1)S(1)}, bf16[1,4096]{1,0:T(2,128)(2,1)S(1)}, u32[]{:S(2)}, u32[]{:S(2)}) %collective-permute-start.9) | collective-permute-done | bytes 8224 | tf_op jit(solution)/shard_map/ppermute | solution.py:66
  84.6 5.8 %collective-permute-done.10 = bf16[1,4096]{1,0:T(2,128)(2,1)S(1)} collective-permute-done((bf16[1,4096]{1,0:T(2,128)(2,1)S(1)}, bf16[1,4096]{1,0:T(2,128)(2,1)S(1)}, u32[]{:S(2)}, u32[]{:S(2)}) %collective-permute-start.10) | collective-permute-done | bytes 8224 | tf_op jit(solution)/shard_map/ppermute | solution.py:66
  90.4 8.5 %gather_fusion = bf16[256,2,16,512]{3,2,1,0:T(8,128)(2,1)} fusion(bf16[64,2,16,512]{3,2,1,0:T(8,128)(2,1)S(1)} %copy-done, s32[1024]{0:T(1024)S(1)} %pad_clamp_fusion), kind=kCustom, calls=%fused_computation | custom fusion | bytes 16778240 | tf_op jit(solution)/shard_map/gather | solution.py:63
  98.8 6.1 %slice_bitcast_fusion = (bf16[16,16,1,16,512]{4,3,1,0,2:T(8,128)(2,1)}, bf16[16,16,1,16,512]{4,3,1,0,2:T(8,128)(2,1)}) fusion(bf16[16,16,2,16,512]{4,3,2,1,0:T(8,128)(2,1)} %bitcast.64), kind=kLoop, calls=%fused_computation.1 | loop fusion | bytes 16777216
  105.6 0.6 fusion.18
  106.2 0.8 dynamic-update-slice
  107.0 0.4 fusion.12
  107.3 12.6 %all-reduce = s32[16]{0:T(128)S(1)} all-reduce(s32[16]{0:T(128)S(1)} %dynamic-update-slice), channel_id=1, replica_groups=mesh['grp'=2,'pool'=16] {'pool'}, use_global_device_ids=true, to_apply=%add | all-reduce | flops 16 | bytes 128
  120.0 6.9 %reshape_squeeze.6 = bf16[16,16,16,4,128]{4,3,2,1,0:T(4,128)(2,1)} reshape(bf16[16,16,1,16,512]{4,3,1,0,2:T(8,128)(2,1)} %get-tuple-element.12) | data formatting | bytes 8388608 | tf_op jit(solution)/shard_map/reshape;squeeze | solution.py:18
  126.9 0.8 concatenate.6
  127.8 12.2 %bitcast_reduce_fusion = (f32[16,16,4,8]{3,1,2,0:T(8,128)S(1)}, f32[16,4,16,16,8]{3,4,2,1,0:T(8,128)S(1)}) fusion(bf16[16,4,8,128,1]{3,2,1,0,4:T(8,128)(2,1)S(1)} %bitcast.66, bf16[16,16,16,4,128]{4,3,2,1,0:T(4,128)(2,1)} %reshape_squeeze.6), kind=kOutput, calls=%fused_computation.4 | convolution fusion | flops 33808384 | bytes 4882432 | tf_op jit(solution)/shard_map/agqd,acbgd->acgqb/dot_general | solution.py:20
  140.0 2.9 %fusion.5 = (f32[16,16,4,8]{3,1,2,0:T(8,128)S(1)}, bf16[16,16,4,8,16]{4,3,1,2,0:T(8,128)(2,1)}) fusion(f32[16,4,16,16,8]{3,4,2,1,0:T(8,128)S(1)} %get-tuple-element.18, f32[16,16,4,8]{3,1,2,0:T(8,128)S(1)} %get-tuple-element.17), kind=kLoop, calls=%fused_computation.11 | loop fusion | flops 516096 | bytes 851968 | tf_op jit(solution)/shard_map/reduce_sum | solution.py:26
  142.9 0.2 select_reduce_fusion
  143.1 0.3 multiply_reduce_fusion.1
  143.5 0.7 copy.55
  144.1 5.8 %all-to-all-start.2 = ((f32[16,1,32]{2,1,0:T(1,128)}), f32[16,1,32]{2,1,0:T(1,128)S(1)}, u32[]{:S(2)}, u32[]{:S(2)}) async-start(f32[16,1,32]{2,1,0:T(1,128)} %copy.55), calls=%async_computation.2 | async-start | bytes 16384 | tf_op jit(solution)/shard_map/all_to_all | solution.py:83
  150.0 6.9 %reshape_squeeze.7 = bf16[16,16,16,4,128]{4,3,2,1,0:T(4,128)(2,1)} reshape(bf16[16,16,1,16,512]{4,3,1,0,2:T(8,128)(2,1)} %get-tuple-element.11) | data formatting | bytes 8388608 | tf_op jit(solution)/shard_map/reshape;squeeze | solution.py:19
  157.0 0.7 copy.47
  157.6 0.2 copy.50
  157.9 6.0 %all-to-all-start = ((f32[16,1,32]{2,1,0:T(1,128)}), f32[16,1,32]{2,1,0:T(1,128)S(1)}, u32[]{:S(2)}, u32[]{:S(2)}) async-start(f32[16,1,32]{2,1,0:T(1,128)} %copy.47), calls=%async_computation | async-start | bytes 16384 | tf_op jit(solution)/shard_map/all_to_all | solution.py:77
  163.9 5.0 %multiply_reduce_fusion = f32[16,4,8,128]{3,2,1,0:T(8,128)} fusion(bf16[16,16,16,4,128]{4,3,2,1,0:T(4,128)(2,1)} %reshape_squeeze.7, bf16[16,16,4,8,16]{4,3,1,2,0:T(8,128)(2,1)} %get-tuple-element.14, f32[16,16,4,8]{3,2,1,0:T(4,128)S(1)} %copy.50), kind=kOutput, calls=%fused_computation.10 | convolution fusion | flops 35586048 | bytes 4751360 | tf_op jit(solution)/shard_map/acgqb,acbgd->acgqd/dot_general | solution.py:27
  168.9 1.3 all-to-all-done
  170.2 4.7 %all-to-all-start.1 = ((f32[16,1,4096]{2,1,0:T(1,128)}), f32[16,1,4096]{2,1,0:T(1,128)S(1)}, u32[]{:S(2)}, u32[]{:S(2)}) async-start(f32[16,1,4096]{2,1,0:T(1,128)} %bitcast.13), calls=%async_computation.1 | async-start | bytes 524288 | tf_op jit(solution)/shard_map/all_to_all | solution.py:80
  175.0 0.1 sub.49
  175.1 0.1 div.21
  175.4 9.5 %all-to-all-done.1 = f32[16,1,4096]{2,1,0:T(1,128)S(1)} async-done(((f32[16,1,4096]{2,1,0:T(1,128)}), f32[16,1,4096]{2,1,0:T(1,128)S(1)}, u32[]{:S(2)}, u32[]{:S(2)}) %all-to-all-start.1) | async-done | bytes 262176 | tf_op jit(solution)/shard_map/all_to_all | solution.py:80
  184.9 0.1 mul.40
  185.1 0.3 multiply_reduce_fusion.2
  185.5 0.5 broadcast.73
  186.0 0.7 reduce.6
  186.7 9.1 %all_to_all.46 = bf16[16,2,128]{2,1,0:T(2,128)(2,1)S(1)} all-to-all(bf16[16,2,128]{2,1,0:T(2,128)(2,1)S(1)} %reshape.153), channel_id=1, replica_groups=mesh['grp'=2,'pool'=16] {'pool'}, dimensions={0} | all-to-all | bytes 16384 | tf_op jit(solution)/shard_map/all_to_all | solution.py:95
  195.8 2.8 %fusion.14 = f32[16,8192]{1,0:T(8,128)S(1)} fusion(bf16[256,8192]{1,0:T(8,128)(2,1)} %param.11, bf16[1,16,256]{2,0,1:T(2,128)(2,1)S(1)} %bitcast.72), kind=kOutput, calls=%fused_computation.30 | convolution fusion | flops 67108864 | bytes 4726784 | tf_op jit(solution)/shard_map/dot_general | solution.py:97
  198.7 63.0 %all-reduce.3 = bf16[16,8192]{1,0:T(8,128)(2,1)S(1)} all-reduce(f32[16,8192]{1,0:T(8,128)S(1)} %fusion.14), channel_id=2, replica_groups=mesh['grp'=2,'pool'=16] {'pool'}, use_global_device_ids=true, to_apply=%region_12.13.clone | all-reduce | flops 131072 | bytes 786432
  261.7 1.3 dynamic-slice_convert_fusion
  (45 shorter events, 0.9 us)
Async XLA Ops:
  0.0 90.4 %copy-start = (bf16[64,2,16,512]{3,2,1,0:T(8,128)(2,1)S(1)}, bf16[64,2,16,512]{3,2,1,0:T(8,128)(2,1)}, u32[]{:S(2)}) copy-start(bf16[64,2,16,512]{3,2,1,0:T(8,128)(2,1)} %param.7) | copy-start | bytes 6291460
  0.0 7.1 %collective-permute-start = (bf16[1,4096]{1,0:T(2,128)(2,1)}, bf16[1,4096]{1,0:T(2,128)(2,1)S(1)}, u32[]{:S(2)}, u32[]{:S(2)}) collective-permute-start(bf16[1,4096]{1,0:T(2,128)(2,1)} %param.6), channel_id=1, source_target_pairs={{0,1},{1,2},{2,3},{3,4},{4,5},{5,6},{6,7},{7,8},{8,9},{9,10},{10,1... | collective-permute-start | bytes 24584 | tf_op jit(solution)/shard_map/ppermute | solution.py:66
  7.1 5.9 %collective-permute-start.1 = (bf16[1,4096]{1,0:T(2,128)(2,1)S(1)}, bf16[1,4096]{1,0:T(2,128)(2,1)S(1)}, u32[]{:S(2)}, u32[]{:S(2)}) collective-permute-start(bf16[1,4096]{1,0:T(2,128)(2,1)S(1)} %collective-permute-done), channel_id=1, source_target_pairs={{0,1},{1,2},{2,3},{3,4},{4,5},{5,6},{6,7},{7,8},{8,9},{9,10},{10,1... | collective-permute-start | bytes 24584 | tf_op jit(solution)/shard_map/ppermute | solution.py:66
  13.0 5.9 %collective-permute-start.2 = (bf16[1,4096]{1,0:T(2,128)(2,1)S(1)}, bf16[1,4096]{1,0:T(2,128)(2,1)S(1)}, u32[]{:S(2)}, u32[]{:S(2)}) collective-permute-start(bf16[1,4096]{1,0:T(2,128)(2,1)S(1)} %collective-permute-done.1), channel_id=1, source_target_pairs={{0,1},{1,2},{2,3},{3,4},{4,5},{5,6},{6,7},{7,8},{8,9},{9,10},{10,1... | collective-permute-start | bytes 24584 | tf_op jit(solution)/shard_map/ppermute | solution.py:66
  18.8 5.9 %collective-permute-start.3 = (bf16[1,4096]{1,0:T(2,128)(2,1)S(1)}, bf16[1,4096]{1,0:T(2,128)(2,1)S(1)}, u32[]{:S(2)}, u32[]{:S(2)}) collective-permute-start(bf16[1,4096]{1,0:T(2,128)(2,1)S(1)} %collective-permute-done.2), channel_id=1, source_target_pairs={{0,1},{1,2},{2,3},{3,4},{4,5},{5,6},{6,7},{7,8},{8,9},{9,10},{10,1... | collective-permute-start | bytes 24584 | tf_op jit(solution)/shard_map/ppermute | solution.py:66
  24.7 5.9 %collective-permute-start.4 = (bf16[1,4096]{1,0:T(2,128)(2,1)S(1)}, bf16[1,4096]{1,0:T(2,128)(2,1)S(1)}, u32[]{:S(2)}, u32[]{:S(2)}) collective-permute-start(bf16[1,4096]{1,0:T(2,128)(2,1)S(1)} %collective-permute-done.3), channel_id=1, source_target_pairs={{0,1},{1,2},{2,3},{3,4},{4,5},{5,6},{6,7},{7,8},{8,9},{9,10},{10,1... | collective-permute-start | bytes 24584 | tf_op jit(solution)/shard_map/ppermute | solution.py:66
  30.6 5.9 %collective-permute-start.5 = (bf16[1,4096]{1,0:T(2,128)(2,1)S(1)}, bf16[1,4096]{1,0:T(2,128)(2,1)S(1)}, u32[]{:S(2)}, u32[]{:S(2)}) collective-permute-start(bf16[1,4096]{1,0:T(2,128)(2,1)S(1)} %collective-permute-done.4), channel_id=1, source_target_pairs={{0,1},{1,2},{2,3},{3,4},{4,5},{5,6},{6,7},{7,8},{8,9},{9,10},{10,1... | collective-permute-start | bytes 24584 | tf_op jit(solution)/shard_map/ppermute | solution.py:66
  36.4 18.2 %collective-permute-start.6 = (bf16[1,4096]{1,0:T(2,128)(2,1)S(1)}, bf16[1,4096]{1,0:T(2,128)(2,1)S(1)}, u32[]{:S(2)}, u32[]{:S(2)}) collective-permute-start(bf16[1,4096]{1,0:T(2,128)(2,1)S(1)} %collective-permute-done.5), channel_id=1, source_target_pairs={{0,1},{1,2},{2,3},{3,4},{4,5},{5,6},{6,7},{7,8},{8,9},{9,10},{10,1... | collective-permute-start | bytes 24584 | tf_op jit(solution)/shard_map/ppermute | solution.py:66
  54.6 5.9 %collective-permute-start.7 = (bf16[1,4096]{1,0:T(2,128)(2,1)S(1)}, bf16[1,4096]{1,0:T(2,128)(2,1)S(1)}, u32[]{:S(2)}, u32[]{:S(2)}) collective-permute-start(bf16[1,4096]{1,0:T(2,128)(2,1)S(1)} %collective-permute-done.6), channel_id=1, source_target_pairs={{0,1},{1,2},{2,3},{3,4},{4,5},{5,6},{6,7},{7,8},{8,9},{9,10},{10,1... | collective-permute-start | bytes 24584 | tf_op jit(solution)/shard_map/ppermute | solution.py:66
  60.4 18.2 %collective-permute-start.8 = (bf16[1,4096]{1,0:T(2,128)(2,1)S(1)}, bf16[1,4096]{1,0:T(2,128)(2,1)S(1)}, u32[]{:S(2)}, u32[]{:S(2)}) collective-permute-start(bf16[1,4096]{1,0:T(2,128)(2,1)S(1)} %collective-permute-done.7), channel_id=1, source_target_pairs={{0,1},{1,2},{2,3},{3,4},{4,5},{5,6},{6,7},{7,8},{8,9},{9,10},{10,1... | collective-permute-start | bytes 24584 | tf_op jit(solution)/shard_map/ppermute | solution.py:66
  78.6 5.9 %collective-permute-start.9 = (bf16[1,4096]{1,0:T(2,128)(2,1)S(1)}, bf16[1,4096]{1,0:T(2,128)(2,1)S(1)}, u32[]{:S(2)}, u32[]{:S(2)}) collective-permute-start(bf16[1,4096]{1,0:T(2,128)(2,1)S(1)} %collective-permute-done.8), channel_id=1, source_target_pairs={{0,1},{1,2},{2,3},{3,4},{4,5},{5,6},{6,7},{7,8},{8,9},{9,10},{10,1... | collective-permute-start | bytes 24584 | tf_op jit(solution)/shard_map/ppermute | solution.py:66
  84.5 5.9 %collective-permute-start.10 = (bf16[1,4096]{1,0:T(2,128)(2,1)S(1)}, bf16[1,4096]{1,0:T(2,128)(2,1)S(1)}, u32[]{:S(2)}, u32[]{:S(2)}) collective-permute-start(bf16[1,4096]{1,0:T(2,128)(2,1)S(1)} %collective-permute-done.9), channel_id=1, source_target_pairs={{0,1},{1,2},{2,3},{3,4},{4,5},{5,6},{6,7},{7,8},{8,9},{9,10},{10,1... | collective-permute-start | bytes 24584 | tf_op jit(solution)/shard_map/ppermute | solution.py:66
  90.3 8.5 %collective-permute-start.11 = (bf16[1,4096]{1,0:T(2,128)(2,1)S(1)}, bf16[1,4096]{1,0:T(2,128)(2,1)S(1)}, u32[]{:S(2)}, u32[]{:S(2)}) collective-permute-start(bf16[1,4096]{1,0:T(2,128)(2,1)S(1)} %collective-permute-done.10), channel_id=1, source_target_pairs={{0,1},{1,2},{2,3},{3,4},{4,5},{5,6},{6,7},{7,8},{8,9},{9,10},{10,1... | collective-permute-start | bytes 24584 | tf_op jit(solution)/shard_map/ppermute | solution.py:66
  98.8 8.1 %collective-permute-start.12 = (bf16[1,4096]{1,0:T(2,128)(2,1)S(1)}, bf16[1,4096]{1,0:T(2,128)(2,1)S(1)}, u32[]{:S(2)}, u32[]{:S(2)}) collective-permute-start(bf16[1,4096]{1,0:T(2,128)(2,1)S(1)} %collective-permute-done.11), channel_id=1, source_target_pairs={{0,1},{1,2},{2,3},{3,4},{4,5},{5,6},{6,7},{7,8},{8,9},{9,10},{10,1... | collective-permute-start | bytes 24584 | tf_op jit(solution)/shard_map/ppermute | solution.py:66
  98.8 6.8 %copy-start.2 = (u32[32]{0:T(128)S(1)}, u32[32]{0:T(128)}, u32[]{:S(2)}) copy-start(u32[32]{0:T(128)} %constant.55) | copy-start | bytes 388
  107.0 12.9 %collective-permute-start.13 = (bf16[1,4096]{1,0:T(2,128)(2,1)S(1)}, bf16[1,4096]{1,0:T(2,128)(2,1)S(1)}, u32[]{:S(2)}, u32[]{:S(2)}) collective-permute-start(bf16[1,4096]{1,0:T(2,128)(2,1)S(1)} %collective-permute-done.12), channel_id=1, source_target_pairs={{0,1},{1,2},{2,3},{3,4},{4,5},{5,6},{6,7},{7,8},{8,9},{9,10},{10,1... | collective-permute-start | bytes 24584 | tf_op jit(solution)/shard_map/ppermute | solution.py:66
  119.9 7.0 %collective-permute-start.14 = (bf16[1,4096]{1,0:T(2,128)(2,1)S(1)}, bf16[1,4096]{1,0:T(2,128)(2,1)S(1)}, u32[]{:S(2)}, u32[]{:S(2)}) collective-permute-start(bf16[1,4096]{1,0:T(2,128)(2,1)S(1)} %collective-permute-done.13), channel_id=1, source_target_pairs={{0,1},{1,2},{2,3},{3,4},{4,5},{5,6},{6,7},{7,8},{8,9},{9,10},{10,1... | collective-permute-start | bytes 24584 | tf_op jit(solution)/shard_map/ppermute | solution.py:66
  120.0 6.9 %copy-start.1 = (bf16[1,4096]{1,0:T(2,128)(2,1)S(1)}, bf16[1,4096]{1,0:T(2,128)(2,1)}, u32[]{:S(2)}) copy-start(bf16[1,4096]{1,0:T(2,128)(2,1)} %param.6) | copy-start | bytes 24580
  144.1 13.7 %all-to-all-start.2 = ((f32[16,1,32]{2,1,0:T(1,128)}), f32[16,1,32]{2,1,0:T(1,128)S(1)}, u32[]{:S(2)}, u32[]{:S(2)}) async-start(f32[16,1,32]{2,1,0:T(1,128)} %copy.55), calls=%async_computation.2 | async-start | bytes 16384 | tf_op jit(solution)/shard_map/all_to_all | solution.py:83
  157.9 12.4 %all-to-all-start = ((f32[16,1,32]{2,1,0:T(1,128)}), f32[16,1,32]{2,1,0:T(1,128)S(1)}, u32[]{:S(2)}, u32[]{:S(2)}) async-start(f32[16,1,32]{2,1,0:T(1,128)} %copy.47), calls=%async_computation | async-start | bytes 16384 | tf_op jit(solution)/shard_map/all_to_all | solution.py:77
  170.2 14.7 %all-to-all-start.1 = ((f32[16,1,4096]{2,1,0:T(1,128)}), f32[16,1,4096]{2,1,0:T(1,128)S(1)}, u32[]{:S(2)}, u32[]{:S(2)}) async-start(f32[16,1,4096]{2,1,0:T(1,128)} %bitcast.13), calls=%async_computation.1 | async-start | bytes 524288 | tf_op jit(solution)/shard_map/all_to_all | solution.py:80
